TPU v7x, 32 devices: a whole 2x2x4 slice. The times are simulated.
32 devices in a mesh: img: 32 (over z, y, x, core).
Axes of the slice: x: 2, y: 2, z: 4, core: 2. Of those that a mesh axis runs over, the one named last changes fastest.
Arguments:
- queries: bfloat16 [12288, 1024], P('img'), may hold values from -10 to 10
- keys: bfloat16 [12288, 1024], P('img'), may hold values from -10 to 10
- values: bfloat16 [12288, 1024], P('img'), may hold values from -6 to 6
- out_grad: bfloat16 [12288, 1024], P('img'), may hold values from -6 to 6
- image_ids: int32 [12288], P('img'), may hold values from 0 to 31, never falling along the last dimension, each value on 1 to 1152 neighbouring positions
Outputs:
- attended: bfloat16 [12288, 1024], P('img')
- query_grad: bfloat16 [12288, 1024], P('img')
- key_grad: bfloat16 [12288, 1024], P('img')
- value_grad: bfloat16 [12288, 1024], P('img')
Inputs may be any that keep to these rules, and one draw needn't show every extreme that they name: `image_ids`: the regions of one image stand in consecutive rows, and ids rise along the rows; an image has 1 to 1152 regions, and some image has exactly 1152.
All inputs are finite; a program needn't handle non-finite values.
Results may differ from a plain program's by a relative error of at most 0.0069.
Values may be sent and summed in bfloat16 or wider, within the bound.
A program may use at most 192 MiB of HBM per device.

v0:
```python
import math

import jax
import jax.numpy as jnp
from jax import lax
from jax.sharding import PartitionSpec as P

D = 1024
HEADS = 16
REACH = 3


def shifted(value, axis, steps):
    count = lax.axis_size(axis)
    leading, last = (max(0, -steps), min(count, count - steps))
    return lax.ppermute(value, axis, [(source, source + steps) for source in range(leading, last)])


def attend_pairs(query_rows, key_rows, value_rows, grad_rows, query_tags, key_tags):
    row_count = query_rows.shape[0]
    width = key_rows.shape[0]
    head_dim = D // HEADS
    pair_cols = 2 * head_dim
    score_scale = 1.0 / math.sqrt(head_dim)
    same_image = (query_tags[:, None] == key_tags[None, :])[None]

    def turn(pair_index, carry):
        attended, query_grad, key_grad, value_grad, peaks, totals, deltas = carry
        start = pair_index * pair_cols
        query_cols = lax.dynamic_slice_in_dim(query_rows, start, pair_cols, 1).reshape(
            row_count, 2, head_dim
        )
        key_cols = lax.dynamic_slice_in_dim(key_rows, start, pair_cols, 1).reshape(
            width, 2, head_dim
        )
        value_cols = lax.dynamic_slice_in_dim(value_rows, start, pair_cols, 1).reshape(
            width, 2, head_dim
        )
        grad_cols = lax.dynamic_slice_in_dim(grad_rows, start, pair_cols, 1).reshape(
            row_count, 2, head_dim
        )
        scores = (
            jnp.einsum("rhd,whd->hrw", query_cols, key_cols, preferred_element_type=jnp.float32)
            * score_scale
        )
        scores = jnp.where(same_image, scores, -1e30)
        peak = jnp.max(scores, axis=-1, keepdims=True)
        weights = jnp.exp(scores - peak)
        total = jnp.sum(weights, axis=-1, keepdims=True)
        probs = weights / total
        probs_b = probs.astype(jnp.bfloat16)
        output = jnp.einsum("hrw,whd->rhd", probs_b, value_cols, preferred_element_type=jnp.float32)
        dprobs = jnp.einsum(
            "rhd,whd->hrw", grad_cols, value_cols, preferred_element_type=jnp.float32
        )
        row_delta = jnp.sum(probs * dprobs, axis=-1, keepdims=True)
        dscores_b = (probs * (dprobs - row_delta)).astype(jnp.bfloat16)
        query_part = (
            jnp.einsum("hrw,whd->rhd", dscores_b, key_cols, preferred_element_type=jnp.float32)
            * score_scale
        )
        attended = lax.dynamic_update_slice_in_dim(
            attended, output.reshape(row_count, pair_cols).astype(jnp.bfloat16), start, 1
        )
        query_grad = lax.dynamic_update_slice_in_dim(
            query_grad, query_part.reshape(row_count, pair_cols).astype(jnp.bfloat16), start, 1
        )
        key_part = (
            jnp.einsum("hrw,rhd->whd", dscores_b, query_cols, preferred_element_type=jnp.float32)
            * score_scale
        )
        value_part = jnp.einsum(
            "hrw,rhd->whd", probs_b, grad_cols, preferred_element_type=jnp.float32
        )
        key_grad = lax.dynamic_update_slice_in_dim(
            key_grad, key_part.reshape(width, pair_cols), start, 1
        )
        value_grad = lax.dynamic_update_slice_in_dim(
            value_grad, value_part.reshape(width, pair_cols), start, 1
        )
        head_start = pair_index * 2
        peaks = lax.dynamic_update_slice_in_dim(peaks, peak[:, :, 0], head_start, 0)
        totals = lax.dynamic_update_slice_in_dim(totals, total[:, :, 0], head_start, 0)
        deltas = lax.dynamic_update_slice_in_dim(deltas, row_delta[:, :, 0], head_start, 0)
        return (attended, query_grad, key_grad, value_grad, peaks, totals, deltas)

    initial = (
        jnp.zeros((row_count, D), jnp.bfloat16),
        jnp.zeros((row_count, D), jnp.bfloat16),
        jnp.zeros((width, D), jnp.float32),
        jnp.zeros((width, D), jnp.float32),
        jnp.zeros((HEADS, row_count), jnp.float32),
        jnp.zeros((HEADS, row_count), jnp.float32),
        jnp.zeros((HEADS, row_count), jnp.float32),
    )
    return lax.fori_loop(0, HEADS // 2, turn, initial)


def fetch_near(block, distance):
    return shifted((block[0], block[1], block[2]), "img", distance)


def return_near(partial_value, distance):
    return shifted((partial_value[0], partial_value[1]), "img", distance)


def shards(queries, keys, values, out_grad, image_ids):
    row_count = queries.shape[0]
    image_tags = image_ids + 1
    own_block = (keys, values, image_tags)
    lower_parts = []
    upper_parts = []
    for offset in range(1, REACH + 1):
        lower_parts.insert(0, fetch_near(own_block, offset))
        upper_parts.append(fetch_near(own_block, -offset))
    all_parts = lower_parts + [own_block] + upper_parts
    window = tuple(
        (jnp.concatenate([piece[member] for piece in all_parts], 0) for member in range(3))
    )
    key_window, value_window, tag_window = window

    def attend_full():
        return attend_pairs(queries, key_window, value_window, out_grad, image_tags, tag_window)

    def attend_near():
        first_row = (REACH - 1) * row_count
        last_row = (REACH + 2) * row_count
        result = attend_pairs(
            queries,
            key_window[first_row:last_row],
            value_window[first_row:last_row],
            out_grad,
            image_tags,
            tag_window[first_row:last_row],
        )
        attended, query_grad, key_grad, value_grad, peaks, totals, deltas = result
        padding = ((first_row, key_window.shape[0] - last_row), (0, 0))
        key_grad = jnp.pad(key_grad, padding)
        value_grad = jnp.pad(value_grad, padding)
        return (attended, query_grad, key_grad, value_grad, peaks, totals, deltas)

    far_needed = jnp.logical_or(
        tag_window[(REACH - 1) * row_count - 1] == image_tags[0],
        tag_window[(REACH + 2) * row_count] == image_tags[row_count - 1],
    )
    result = lax.cond(far_needed, attend_full, attend_near)
    attended, query_grad, key_part, value_part, peaks, totals, deltas = result
    own_start = REACH * row_count
    key_total = key_part[own_start : own_start + row_count]
    value_total = value_part[own_start : own_start + row_count]
    for offset in range(-REACH, REACH + 1):
        if offset != 0:
            begin = (offset + REACH) * row_count
            key_back, value_back = return_near(
                (key_part[begin : begin + row_count], value_part[begin : begin + row_count]), offset
            )
            key_total = key_total + key_back
            value_total = value_total + value_back
    return (attended, query_grad, key_total.astype(jnp.bfloat16), value_total.astype(jnp.bfloat16))


def solution(mesh):
    in_specs = (P("img", None), P("img", None), P("img", None), P("img", None), P("img"))
    out_specs = (P("img", None), P("img", None), P("img", None), P("img", None))
    return jax.shard_map(shards, mesh=mesh, in_specs=in_specs, out_specs=out_specs, check_vma=False)
```

profile of v0, /device:TPU:0, one launch (start us, length us, event | category | flops | bytes accessed | tf_op | source)
XLA Modules:
  0.0 750.1 jit_solution(13794852221198306976)
XLA Ops:
  3.9 3.0 collective-permute-start.15
  6.9 7.1 collective-permute-start.14
  14.0 4.2 collective-permute-start
  21.8 2.6 collective-permute-start.2
  24.5 3.8 collective-permute-start.4
  28.3 2.5 collective-permute-start.3
  32.8 4.5 collective-permute-start.8
  37.3 20.8 %collective-permute-done.1 = s32[384]{0:T(512)S(1)} collective-permute-done((s32[384]{0:T(512)S(1)}, s32[384]{0:T(512)S(1)}, u32[]{:S(2)}, u32[]{:S(2)}) %collective-permute-start.1) | collective-permute-done | bytes 1568 | tf_op jit(solution)/shard_map/ppermute | solution.py:16
  58.1 4.7 collective-permute-start.9
  66.6 29.3 %collective-permute-start.10 = (bf16[384,1024]{0,1:T(8,128)(2,1)S(1)}, bf16[384,1024]{0,1:T(8,128)(2,1)S(1)}, u32[]{:S(2)}, u32[]{:S(2)}) collective-permute-start(bf16[384,1024]{0,1:T(8,128)(2,1)S(1)} %copy.16), channel_id=1, source_target_pairs={{0,1},{1,2},{2,3},{3,4},{4,5},{5,6},{6,7},{7,8},{8,9},{9,10},{10,1... | collective-permute-start | bytes 2359304 | tf_op jit(solution)/shard_map/ppermute | solution.py:16
  113.0 22.6 %collective-permute-done.6 = bf16[384,1024]{0,1:T(8,128)(2,1)S(1)} collective-permute-done((bf16[384,1024]{0,1:T(8,128)(2,1)S(1)}, bf16[384,1024]{0,1:T(8,128)(2,1)S(1)}, u32[]{:S(2)}, u32[]{:S(2)}) %collective-permute-start.6) | collective-permute-done | bytes 786464 | tf_op jit(solution)/shard_map/ppermute | solution.py:16
  136.7 13.3 %collective-permute-done.7 = bf16[384,1024]{0,1:T(8,128)(2,1)S(1)} collective-permute-done((bf16[384,1024]{0,1:T(8,128)(2,1)S(1)}, bf16[384,1024]{0,1:T(8,128)(2,1)S(1)}, u32[]{:S(2)}, u32[]{:S(2)}) %collective-permute-start.7) | collective-permute-done | bytes 786464 | tf_op jit(solution)/shard_map/ppermute | solution.py:16
  151.9 17.4 %collective-permute-done.12 = bf16[384,1024]{0,1:T(8,128)(2,1)S(1)} collective-permute-done((bf16[384,1024]{0,1:T(8,128)(2,1)S(1)}, bf16[384,1024]{0,1:T(8,128)(2,1)S(1)}, u32[]{:S(2)}, u32[]{:S(2)}) %collective-permute-start.12) | collective-permute-done | bytes 786464 | tf_op jit(solution)/shard_map/ppermute | solution.py:16
  170.4 6.1 collective-permute-done.13
  177.5 205.4 %conditional.1 = (bf16[384,1024]{0,1:T(8,128)(2,1)}, bf16[384,1024]{0,1:T(8,128)(2,1)}, f32[2688,1024]{0,1:T(8,128)}, f32[2688,1024]{0,1:T(8,128)}) conditional(s32[]{:T(128)} %bitcast, (bf16[2688,1024]{0,1:T(8,128)(2,1)}, bf16[2688,1024]{0,1:T(8,128)(2,1)}, s32[384]{0:T(512)S(1)}, s32[2688]{0:T(1024)S(1)}, bf16[384,1024]{1,0:T(8,128)(2,1)}, ...), branch_computations={%region_0.6_spmd, %region_6.12_spmd} | conditional | flops 2158813696 | bytes 127279744 | solution.py:146
  179.4 3.2 slice.44
  184.5 2.5 broadcast.138.clone
  187.0 2.4 broadcast.138
  189.4 181.5 %while.38 = (s32[]{:T(128)}, bf16[384,1024]{0,1:T(8,128)(2,1)}, bf16[384,1024]{0,1:T(8,128)(2,1)}, f32[1152,1024]{0,1:T(8,128)}, f32[1152,1024]{0,1:T(8,128)}, /...) while((s32[]{:T(128)}, bf16[384,1024]{0,1:T(8,128)(2,1)}, ...), condition=%wide.region_5.5_spmd.clone, body=%wide.region_1.4_spmd.clone.sunk | while | flops 925290624 | bytes 56491444 | solution.py:96
  196.4 2.7 fusion.152
  199.0 3.6 convolution_convert_fusion.2
  202.6 3.7 fusion.154
  219.1 2.7 fusion.152
  221.7 3.6 convolution_convert_fusion.2
  225.3 3.7 fusion.154
  241.8 2.7 fusion.152
  244.4 3.6 convolution_convert_fusion.2
  248.0 3.7 fusion.154
  264.4 2.7 fusion.152
  267.1 3.6 convolution_convert_fusion.2
  270.7 3.7 fusion.154
  287.1 2.7 fusion.152
  289.8 3.6 convolution_convert_fusion.2
  293.4 3.7 fusion.154
  309.8 2.7 fusion.152
  312.5 3.6 convolution_convert_fusion.2
  316.1 3.7 fusion.154
  332.5 2.7 fusion.152
  335.1 3.6 convolution_convert_fusion.2
  338.7 3.7 fusion.154
  355.2 2.7 fusion.152
  357.9 3.6 convolution_convert_fusion.2
  361.5 3.7 fusion.154
  370.9 7.2 pad.6
  378.1 4.8 pad.5
  382.9 12.1 %copy.27 = f32[2688,1024]{1,0:T(8,128)} copy(f32[2688,1024]{0,1:T(8,128)} %get-tuple-element.390) | data formatting | bytes 22020096 | tf_op jit(solution)/shard_map/cond | solution.py:146
  395.0 7.8 %fusion.47 = (f32[384,1024]{1,0:T(8,128)}, f32[384,1024]{1,0:T(8,128)}, f32[384,1024]{1,0:T(8,128)}, f32[384,1024]{1,0:T(8,128)}, f32[384,1024]{1,0:T(8,128)}, /*index=5*/f32[384,1024]{1,0:T(8,128)}) fusion(f32[2688,1024]{1,0:T(8,128)} %copy.27), kind=kLoop, calls=%fused_computation.98 | loop fusion | bytes 18874368 | tf_op jit(solution)/shard_map/slice | solution.py:155
  404.1 56.6 %collective-permute-start.23 = (f32[384,1024]{1,0:T(8,128)}, f32[384,1024]{1,0:T(8,128)}, u32[]{:S(2)}, u32[]{:S(2)}) collective-permute-start(f32[384,1024]{1,0:T(8,128)} %get-tuple-element.527), channel_id=1, source_target_pairs={{0,3},{1,4},{2,5},{3,6},{4,7},{5,8},{6,9},{7,10},{8,11},{9,12},{10... | collective-permute-start | bytes 4718600 | tf_op jit(solution)/shard_map/ppermute | solution.py:16
  460.6 17.5 %collective-permute-start.22 = (f32[384,1024]{1,0:T(8,128)}, f32[384,1024]{1,0:T(8,128)}, u32[]{:S(2)}, u32[]{:S(2)}) collective-permute-start(f32[384,1024]{1,0:T(8,128)} %get-tuple-element.528), channel_id=1, source_target_pairs={{0,2},{1,3},{2,4},{3,5},{4,6},{5,7},{6,8},{7,9},{8,10},{9,11},{10,... | collective-permute-start | bytes 4718600 | tf_op jit(solution)/shard_map/ppermute | solution.py:16
  478.1 2.5 collective-permute-start.21
  481.9 12.1 %copy.34 = f32[2688,1024]{1,0:T(8,128)} copy(f32[2688,1024]{0,1:T(8,128)} %get-tuple-element.391) | data formatting | bytes 22020096 | tf_op jit(solution)/shard_map/cond | solution.py:146
  494.0 6.8 fusion.46
  502.1 4.2 collective-permute-done.23
  507.6 78.0 %collective-permute-done.22 = f32[384,1024]{1,0:T(8,128)} collective-permute-done((f32[384,1024]{1,0:T(8,128)}, f32[384,1024]{1,0:T(8,128)}, u32[]{:S(2)}, u32[]{:S(2)}) %collective-permute-start.22) | collective-permute-done | bytes 1572896 | tf_op jit(solution)/shard_map/ppermute | solution.py:16
  585.6 2.4 collective-permute-start.29
  588.1 26.8 %collective-permute-start.28 = (f32[384,1024]{1,0:T(8,128)}, f32[384,1024]{1,0:T(8,128)}, u32[]{:S(2)}, u32[]{:S(2)}) collective-permute-start(f32[384,1024]{1,0:T(8,128)} %get-tuple-element.522), channel_id=1, source_target_pairs={{0,2},{1,3},{2,4},{3,5},{4,6},{5,7},{6,8},{7,9},{8,10},{9,11},{10,... | collective-permute-start | bytes 4718600 | tf_op jit(solution)/shard_map/ppermute | solution.py:16
  614.9 2.4 collective-permute-start.27
  617.3 6.2 collective-permute-done.19
  624.8 4.4 collective-permute-done.24
  635.0 6.2 fusion.43
  641.3 51.5 %collective-permute-done.29 = f32[384,1024]{1,0:T(8,128)} collective-permute-done((f32[384,1024]{1,0:T(8,128)}, f32[384,1024]{1,0:T(8,128)}, u32[]{:S(2)}, u32[]{:S(2)}) %collective-permute-start.29) | collective-permute-done | bytes 1572896 | tf_op jit(solution)/shard_map/ppermute | solution.py:16
  692.8 33.7 %collective-permute-done.28 = f32[384,1024]{1,0:T(8,128)} collective-permute-done((f32[384,1024]{1,0:T(8,128)}, f32[384,1024]{1,0:T(8,128)}, u32[]{:S(2)}, u32[]{:S(2)}) %collective-permute-start.28) | collective-permute-done | bytes 1572896 | tf_op jit(solution)/shard_map/ppermute | solution.py:16
  726.5 17.9 %collective-permute-done.25 = f32[384,1024]{1,0:T(8,128)} collective-permute-done((f32[384,1024]{1,0:T(8,128)S(1)}, f32[384,1024]{1,0:T(8,128)}, u32[]{:S(2)}, u32[]{:S(2)}) %collective-permute-start.25) | collective-permute-done | bytes 1572896 | tf_op jit(solution)/shard_map/ppermute | solution.py:16
  744.4 5.7 fusion.37
  (309 shorter events, 149.3 us)
Async XLA Ops:
  1.3 30.2 %collective-permute-start.17 = (s32[384]{0:T(512)S(1)}, s32[384]{0:T(512)S(1)}, u32[]{:S(2)}, u32[]{:S(2)}) collective-permute-start(s32[384]{0:T(512)S(1)} %broadcast_add_fusion), channel_id=1, source_target_pairs={{3,0},{4,1},{5,2},{6,3},{7,4},{8,5},{9,6},{10,7},{11,8},{12,9},{13... | collective-permute-start | bytes 4616 | tf_op jit(solution)/shard_map/ppermute | solution.py:16
  2.6 30.2 %collective-permute-start.16 = (s32[384]{0:T(512)S(1)}, s32[384]{0:T(512)S(1)}, u32[]{:S(2)}, u32[]{:S(2)}) collective-permute-start(s32[384]{0:T(512)S(1)} %broadcast_add_fusion), channel_id=1, source_target_pairs={{1,0},{2,1},{3,2},{4,3},{5,4},{6,5},{7,6},{8,7},{9,8},{10,9},{11,1... | collective-permute-start | bytes 4616 | tf_op jit(solution)/shard_map/ppermute | solution.py:16
  3.9 24.4 %collective-permute-start.15 = (s32[384]{0:T(512)S(1)}, s32[384]{0:T(512)S(1)}, u32[]{:S(2)}, u32[]{:S(2)}) collective-permute-start(s32[384]{0:T(512)S(1)} %broadcast_add_fusion), channel_id=1, source_target_pairs={{0,1},{1,2},{2,3},{3,4},{4,5},{5,6},{6,7},{7,8},{8,9},{9,10},{10,1... | collective-permute-start | bytes 4616 | tf_op jit(solution)/shard_map/ppermute | solution.py:16
  6.9 14.9 %collective-permute-start.14 = (s32[384]{0:T(512)S(1)}, s32[384]{0:T(512)S(1)}, u32[]{:S(2)}, u32[]{:S(2)}) collective-permute-start(s32[384]{0:T(512)S(1)} %broadcast_add_fusion), channel_id=1, source_target_pairs={{0,3},{1,4},{2,5},{3,6},{4,7},{5,8},{6,9},{7,10},{8,11},{9,12},{10... | collective-permute-start | bytes 4616 | tf_op jit(solution)/shard_map/ppermute | solution.py:16
  14.0 10.4 %collective-permute-start = (s32[384]{0:T(512)S(1)}, s32[384]{0:T(512)S(1)}, u32[]{:S(2)}, u32[]{:S(2)}) collective-permute-start(s32[384]{0:T(512)S(1)} %broadcast_add_fusion), channel_id=1, source_target_pairs={{0,2},{1,3},{2,4},{3,5},{4,6},{5,7},{6,8},{7,9},{8,10},{9,11},{10,... | collective-permute-start | bytes 4616 | tf_op jit(solution)/shard_map/ppermute | solution.py:16
  21.8 44.8 %collective-permute-start.2 = (bf16[384,1024]{0,1:T(8,128)(2,1)S(1)}, bf16[384,1024]{0,1:T(8,128)(2,1)S(1)}, u32[]{:S(2)}, u32[]{:S(2)}) collective-permute-start(bf16[384,1024]{0,1:T(8,128)(2,1)S(1)} %copy.9), channel_id=1, source_target_pairs={{0,3},{1,4},{2,5},{3,6},{4,7},{5,8},{6,9},{7,10},{8,11},{9,12},{10... | collective-permute-start | bytes 2359304 | tf_op jit(solution)/shard_map/ppermute | solution.py:16
  24.5 74.7 %collective-permute-start.4 = (bf16[384,1024]{0,1:T(8,128)(2,1)S(1)}, bf16[384,1024]{0,1:T(8,128)(2,1)S(1)}, u32[]{:S(2)}, u32[]{:S(2)}) collective-permute-start(bf16[384,1024]{0,1:T(8,128)(2,1)S(1)} %copy.9), channel_id=1, source_target_pairs={{0,1},{1,2},{2,3},{3,4},{4,5},{5,6},{6,7},{7,8},{8,9},{9,10},{10,1... | collective-permute-start | bytes 2359304 | tf_op jit(solution)/shard_map/ppermute | solution.py:16
  28.3 68.6 %collective-permute-start.3 = (bf16[384,1024]{0,1:T(8,128)(2,1)S(1)}, bf16[384,1024]{0,1:T(8,128)(2,1)S(1)}, u32[]{:S(2)}, u32[]{:S(2)}) collective-permute-start(bf16[384,1024]{0,1:T(8,128)(2,1)S(1)} %copy.9), channel_id=1, source_target_pairs={{0,2},{1,3},{2,4},{3,5},{4,6},{5,7},{6,8},{7,9},{8,10},{9,11},{10,... | collective-permute-start | bytes 2359304 | tf_op jit(solution)/shard_map/ppermute | solution.py:16
  31.5 26.6 %collective-permute-start.1 = (s32[384]{0:T(512)S(1)}, s32[384]{0:T(512)S(1)}, u32[]{:S(2)}, u32[]{:S(2)}) collective-permute-start(s32[384]{0:T(512)S(1)} %broadcast_add_fusion), channel_id=1, source_target_pairs={{2,0},{3,1},{4,2},{5,3},{6,4},{7,5},{8,6},{9,7},{10,8},{11,9},{12,... | collective-permute-start | bytes 4616 | tf_op jit(solution)/shard_map/ppermute | solution.py:16
  32.8 69.8 %collective-permute-start.8 = (bf16[384,1024]{0,1:T(8,128)(2,1)S(1)}, bf16[384,1024]{0,1:T(8,128)(2,1)S(1)}, u32[]{:S(2)}, u32[]{:S(2)}) collective-permute-start(bf16[384,1024]{0,1:T(8,128)(2,1)S(1)} %copy.16), channel_id=1, source_target_pairs={{0,3},{1,4},{2,5},{3,6},{4,7},{5,8},{6,9},{7,10},{8,11},{9,12},{10... | collective-permute-start | bytes 2359304 | tf_op jit(solution)/shard_map/ppermute | solution.py:16
  58.1 46.9 %collective-permute-start.9 = (bf16[384,1024]{0,1:T(8,128)(2,1)S(1)}, bf16[384,1024]{0,1:T(8,128)(2,1)S(1)}, u32[]{:S(2)}, u32[]{:S(2)}) collective-permute-start(bf16[384,1024]{0,1:T(8,128)(2,1)S(1)} %copy.16), channel_id=1, source_target_pairs={{0,2},{1,3},{2,4},{3,5},{4,6},{5,7},{6,8},{7,9},{8,10},{9,11},{10,... | collective-permute-start | bytes 2359304 | tf_op jit(solution)/shard_map/ppermute | solution.py:16
  66.6 40.7 %collective-permute-start.10 = (bf16[384,1024]{0,1:T(8,128)(2,1)S(1)}, bf16[384,1024]{0,1:T(8,128)(2,1)S(1)}, u32[]{:S(2)}, u32[]{:S(2)}) collective-permute-start(bf16[384,1024]{0,1:T(8,128)(2,1)S(1)} %copy.16), channel_id=1, source_target_pairs={{0,1},{1,2},{2,3},{3,4},{4,5},{5,6},{6,7},{7,8},{8,9},{9,10},{10,1... | collective-permute-start | bytes 2359304 | tf_op jit(solution)/shard_map/ppermute | solution.py:16
  96.9 12.7 %collective-permute-start.5 = (bf16[384,1024]{0,1:T(8,128)(2,1)S(1)}, bf16[384,1024]{0,1:T(8,128)(2,1)S(1)}, u32[]{:S(2)}, u32[]{:S(2)}) collective-permute-start(bf16[384,1024]{0,1:T(8,128)(2,1)S(1)} %copy.9), channel_id=1, source_target_pairs={{1,0},{2,1},{3,2},{4,3},{5,4},{6,5},{7,6},{8,7},{9,8},{10,9},{11,1... | collective-permute-start | bytes 2359304 | tf_op jit(solution)/shard_map/ppermute | solution.py:16
  99.2 36.4 %collective-permute-start.6 = (bf16[384,1024]{0,1:T(8,128)(2,1)S(1)}, bf16[384,1024]{0,1:T(8,128)(2,1)S(1)}, u32[]{:S(2)}, u32[]{:S(2)}) collective-permute-start(bf16[384,1024]{0,1:T(8,128)(2,1)S(1)} %copy.9), channel_id=1, source_target_pairs={{2,0},{3,1},{4,2},{5,3},{6,4},{7,5},{8,6},{9,7},{10,8},{11,9},{12,... | collective-permute-start | bytes 2359304 | tf_op jit(solution)/shard_map/ppermute | solution.py:16
  102.6 47.3 %collective-permute-start.7 = (bf16[384,1024]{0,1:T(8,128)(2,1)S(1)}, bf16[384,1024]{0,1:T(8,128)(2,1)S(1)}, u32[]{:S(2)}, u32[]{:S(2)}) collective-permute-start(bf16[384,1024]{0,1:T(8,128)(2,1)S(1)} %copy.9), channel_id=1, source_target_pairs={{3,0},{4,1},{5,2},{6,3},{7,4},{8,5},{9,6},{10,7},{11,8},{12,9},{13... | collective-permute-start | bytes 2359304 | tf_op jit(solution)/shard_map/ppermute | solution.py:16
  105.0 46.0 %collective-permute-start.11 = (bf16[384,1024]{0,1:T(8,128)(2,1)S(1)}, bf16[384,1024]{0,1:T(8,128)(2,1)S(1)}, u32[]{:S(2)}, u32[]{:S(2)}) collective-permute-start(bf16[384,1024]{0,1:T(8,128)(2,1)S(1)} %copy.16), channel_id=1, source_target_pairs={{1,0},{2,1},{3,2},{4,3},{5,4},{6,5},{7,6},{8,7},{9,8},{10,9},{11,1... | collective-permute-start | bytes 2359304 | tf_op jit(solution)/shard_map/ppermute | solution.py:16
  107.3 62.0 %collective-permute-start.12 = (bf16[384,1024]{0,1:T(8,128)(2,1)S(1)}, bf16[384,1024]{0,1:T(8,128)(2,1)S(1)}, u32[]{:S(2)}, u32[]{:S(2)}) collective-permute-start(bf16[384,1024]{0,1:T(8,128)(2,1)S(1)} %copy.16), channel_id=1, source_target_pairs={{2,0},{3,1},{4,2},{5,3},{6,4},{7,5},{8,6},{9,7},{10,8},{11,9},{12,... | collective-permute-start | bytes 2359304 | tf_op jit(solution)/shard_map/ppermute | solution.py:16
  109.6 66.9 %collective-permute-start.13 = (bf16[384,1024]{0,1:T(8,128)(2,1)S(1)}, bf16[384,1024]{0,1:T(8,128)(2,1)S(1)}, u32[]{:S(2)}, u32[]{:S(2)}) collective-permute-start(bf16[384,1024]{0,1:T(8,128)(2,1)S(1)} %copy.16), channel_id=1, source_target_pairs={{3,0},{4,1},{5,2},{6,3},{7,4},{8,5},{9,6},{10,7},{11,8},{12,9},{13... | collective-permute-start | bytes 2359304 | tf_op jit(solution)/shard_map/ppermute | solution.py:16
  189.4 5.8 copy-start.5
  189.4 5.8 copy-start.12
  209.1 3.0 copy-start.6
  209.1 3.0 copy-start.13
  212.1 5.9 copy-start.5
  212.1 5.9 copy-start.12
  231.8 3.0 copy-start.6
  231.8 3.0 copy-start.13
  234.8 5.9 copy-start.5
  234.8 5.9 copy-start.12
  254.5 3.0 copy-start.6
  254.5 3.0 copy-start.13
  257.5 5.9 copy-start.5
  257.5 5.9 copy-start.12
  277.2 3.0 copy-start.6
  277.2 3.0 copy-start.13
  280.2 5.9 copy-start.5
  280.2 5.9 copy-start.12
  299.9 3.0 copy-start.6
  299.9 3.0 copy-start.13
  302.8 5.9 copy-start.5
  302.8 5.9 copy-start.12
  325.5 5.9 copy-start.5
  325.5 5.9 copy-start.12
  345.2 3.0 copy-start.6
  345.2 3.0 copy-start.13
  348.2 5.9 copy-start.5
  348.2 5.9 copy-start.12
  367.9 3.0 copy-start.6
  367.9 3.0 copy-start.13
  370.9 7.2 copy-start.1
  402.8 98.0 %collective-permute-start.18 = (f32[384,1024]{1,0:T(8,128)}, f32[384,1024]{1,0:T(8,128)}, u32[]{:S(2)}, u32[]{:S(2)}) collective-permute-start(f32[384,1024]{1,0:T(8,128)} %get-tuple-element.526), channel_id=1, source_target_pairs={{3,0},{4,1},{5,2},{6,3},{7,4},{8,5},{9,6},{10,7},{11,8},{12,9},{13... | collective-permute-start | bytes 4718600 | tf_op jit(solution)/shard_map/ppermute | solution.py:16
  404.1 102.3 %collective-permute-start.23 = (f32[384,1024]{1,0:T(8,128)}, f32[384,1024]{1,0:T(8,128)}, u32[]{:S(2)}, u32[]{:S(2)}) collective-permute-start(f32[384,1024]{1,0:T(8,128)} %get-tuple-element.527), channel_id=1, source_target_pairs={{0,3},{1,4},{2,5},{3,6},{4,7},{5,8},{6,9},{7,10},{8,11},{9,12},{10... | collective-permute-start | bytes 4718600 | tf_op jit(solution)/shard_map/ppermute | solution.py:16
  460.6 125.0 %collective-permute-start.22 = (f32[384,1024]{1,0:T(8,128)}, f32[384,1024]{1,0:T(8,128)}, u32[]{:S(2)}, u32[]{:S(2)}) collective-permute-start(f32[384,1024]{1,0:T(8,128)} %get-tuple-element.528), channel_id=1, source_target_pairs={{0,2},{1,3},{2,4},{3,5},{4,6},{5,7},{6,8},{7,9},{8,10},{9,11},{10,... | collective-permute-start | bytes 4718600 | tf_op jit(solution)/shard_map/ppermute | solution.py:16
  478.1 110.0 %collective-permute-start.21 = (f32[384,1024]{1,0:T(8,128)}, f32[384,1024]{1,0:T(8,128)}, u32[]{:S(2)}, u32[]{:S(2)}) collective-permute-start(f32[384,1024]{1,0:T(8,128)} %get-tuple-element.529), channel_id=1, source_target_pairs={{0,1},{1,2},{2,3},{3,4},{4,5},{5,6},{6,7},{7,8},{8,9},{9,10},{10,1... | collective-permute-start | bytes 4718600 | tf_op jit(solution)/shard_map/ppermute | solution.py:16
  480.6 134.3 %collective-permute-start.20 = (f32[384,1024]{1,0:T(8,128)}, f32[384,1024]{1,0:T(8,128)}, u32[]{:S(2)}, u32[]{:S(2)}) collective-permute-start(f32[384,1024]{1,0:T(8,128)} %get-tuple-element.530), channel_id=1, source_target_pairs={{1,0},{2,1},{3,2},{4,3},{5,4},{6,5},{7,6},{8,7},{9,8},{10,9},{11,1... | collective-permute-start | bytes 4718600 | tf_op jit(solution)/shard_map/ppermute | solution.py:16
  494.0 6.8 copy-start.8
  500.8 122.7 %collective-permute-start.19 = (f32[384,1024]{1,0:T(8,128)S(1)}, f32[384,1024]{1,0:T(8,128)S(1)}, u32[]{:S(2)}, u32[]{:S(2)}) collective-permute-start(f32[384,1024]{1,0:T(8,128)S(1)} %copy-done.8), channel_id=1, source_target_pairs={{2,0},{3,1},{4,2},{5,3},{6,4},{7,5},{8,6},{9,7},{10,8},{11,9},{12,... | collective-permute-start | bytes 4718600 | tf_op jit(solution)/shard_map/ppermute | solution.py:16
  506.3 122.8 %collective-permute-start.24 = (f32[384,1024]{1,0:T(8,128)S(1)}, f32[384,1024]{1,0:T(8,128)S(1)}, u32[]{:S(2)}, u32[]{:S(2)}) collective-permute-start(f32[384,1024]{1,0:T(8,128)S(1)} %get-tuple-element.520), channel_id=1, source_target_pairs={{3,0},{4,1},{5,2},{6,3},{7,4},{8,5},{9,6},{10,7},{11,8},{12,9},{13... | collective-permute-start | bytes 4718600 | tf_op jit(solution)/shard_map/ppermute | solution.py:16
  585.6 107.2 %collective-permute-start.29 = (f32[384,1024]{1,0:T(8,128)}, f32[384,1024]{1,0:T(8,128)}, u32[]{:S(2)}, u32[]{:S(2)}) collective-permute-start(f32[384,1024]{1,0:T(8,128)} %get-tuple-element.521), channel_id=1, source_target_pairs={{0,3},{1,4},{2,5},{3,6},{4,7},{5,8},{6,9},{7,10},{8,11},{9,12},{10... | collective-permute-start | bytes 4718600 | tf_op jit(solution)/shard_map/ppermute | solution.py:16
  588.1 138.4 %collective-permute-start.28 = (f32[384,1024]{1,0:T(8,128)}, f32[384,1024]{1,0:T(8,128)}, u32[]{:S(2)}, u32[]{:S(2)}) collective-permute-start(f32[384,1024]{1,0:T(8,128)} %get-tuple-element.522), channel_id=1, source_target_pairs={{0,2},{1,3},{2,4},{3,5},{4,6},{5,7},{6,8},{7,9},{8,10},{9,11},{10,... | collective-permute-start | bytes 4718600 | tf_op jit(solution)/shard_map/ppermute | solution.py:16
  614.9 111.7 %collective-permute-start.27 = (f32[384,1024]{1,0:T(8,128)}, f32[384,1024]{1,0:T(8,128)}, u32[]{:S(2)}, u32[]{:S(2)}) collective-permute-start(f32[384,1024]{1,0:T(8,128)} %get-tuple-element.523), channel_id=1, source_target_pairs={{0,1},{1,2},{2,3},{3,4},{4,5},{5,6},{6,7},{7,8},{8,9},{9,10},{10,1... | collective-permute-start | bytes 4718600 | tf_op jit(solution)/shard_map/ppermute | solution.py:16
  623.5 7.0 copy-start.11
  623.5 103.0 %collective-permute-start.26 = (f32[384,1024]{1,0:T(8,128)S(1)}, f32[384,1024]{1,0:T(8,128)}, u32[]{:S(2)}, u32[]{:S(2)}) collective-permute-start(f32[384,1024]{1,0:T(8,128)S(1)} %get-tuple-element.524), channel_id=1, source_target_pairs={{1,0},{2,1},{3,2},{4,3},{5,4},{6,5},{7,6},{8,7},{9,8},{10,9},{11,1... | collective-permute-start | bytes 4718600 | tf_op jit(solution)/shard_map/ppermute | solution.py:16
  629.1 115.2 %collective-permute-start.25 = (f32[384,1024]{1,0:T(8,128)S(1)}, f32[384,1024]{1,0:T(8,128)}, u32[]{:S(2)}, u32[]{:S(2)}) collective-permute-start(f32[384,1024]{1,0:T(8,128)S(1)} %get-tuple-element.525), channel_id=1, source_target_pairs={{2,0},{3,1},{4,2},{5,3},{6,4},{7,5},{8,6},{9,7},{10,8},{11,9},{12,... | collective-permute-start | bytes 4718600 | tf_op jit(solution)/shard_map/ppermute | solution.py:16
  635.0 109.4 %copy-start.10 = (f32[384,1024]{1,0:T(8,128)S(1)}, f32[384,1024]{1,0:T(8,128)}, u32[]{:S(2)}) copy-start(f32[384,1024]{1,0:T(8,128)} %copy-done.9) | copy-start | bytes 4718596
  (35 other events, 52.2 us)
where the time goes:
time: 753 us; the launch traced here: 750 us
  waiting for transfers between devices  276 us (37%)
  starting transfers between devices  189 us (25%)
  local copies, waits for them, and re-layouts  151 us (20%)
  matrix products  103 us (14%)
  other arithmetic  26.6 us (4%)
    ppermute x30, waiting for transfers between devices, shifted(): lax.ppermute(value, axis, [(source, source + steps) for source in range(l...  276 us
    ppermute x30, starting transfers between devices, shifted(): lax.ppermute(value, axis, [(source, source + steps) for source in range(l...  189 us
    dot_general x8, matrix products, turn(): jnp.einsum('hrw,rhd->whd', probs_b, grad_cols, preferred_element_type=jnp...  29.7 us
    dot_general x8, matrix products, turn(): jnp.einsum('hrw,whd->rhd', probs_b, value_cols, preferred_element_type=jn...  28.7 us
    cond x2, local copies, waits for them, and re-layouts, shards(): result = lax.cond(far_needed, attend_full, attend_near)  24.2 us
    sub x8, matrix products, turn(): weights = jnp.exp(scores - peak)  21.3 us
    unnamed x29, local copies, waits for them, and re-layouts  20.1 us
  transfers between devices with their start and end apart: 30, of which 12 were waited for; matrix products, arithmetic and copies ran while one was open for 6% of the time, Pallas kernels for 0%

commit v1 on v0

v1 whole, which is shorter than its diff:
```python
import math

import jax
import jax.numpy as jnp
from jax import lax
from jax.experimental import pallas as pl
from jax.experimental.pallas import tpu as pltpu
from jax.sharding import PartitionSpec as P

HEAD_DIM = 64
REACH = 3
LANES = 128
TQ = 128
TK = 256
NO_TAG = 1 << 30


def dot_nt(a, b):
    return lax.dot_general(a, b, (((1,), (1,)), ((), ())), preferred_element_type=jnp.float32)


def dot_nn(a, b):
    return lax.dot_general(a, b, (((1,), (0,)), ((), ())), preferred_element_type=jnp.float32)


def attend_kernel(
    tags_s, bounds, q_ref, k_ref, v_ref, g_ref, kt_ref, vt_ref, tag_cols, tag_rows,
    att_ref, dq_ref, dk_ref, dv_ref,
    s_buf, dp_buf, dk_acc, dv_acc, att_acc, dq_acc,
):
    dk_acc[...] = jnp.zeros_like(dk_acc)
    dv_acc[...] = jnp.zeros_like(dv_acc)
    low = lax.broadcasted_iota(jnp.int32, (TQ, LANES), 1) < HEAD_DIM
    scale = 1.0 / math.sqrt(HEAD_DIM)
    all_tags = tag_rows[...]

    def one_tile(tile, carry):
        row0 = pl.multiple_of(tile * TQ, TQ)
        rows = pl.ds(row0, TQ)
        first_tag = tags_s[row0]
        last_tag = tags_s[row0 + TQ - 1]
        key_begin = jnp.sum((all_tags < first_tag).astype(jnp.int32))
        key_end = jnp.sum((all_tags <= last_tag).astype(jnp.int32))
        key0 = (key_begin // LANES) * LANES
        steps = (key_end - key0 + TK - 1) // TK
        q = q_ref[rows, :].astype(jnp.float32) * scale
        g = g_ref[rows, :].astype(jnp.float32)
        q2 = jnp.concatenate(
            [jnp.where(low, q, 0.0), jnp.where(low, 0.0, q)], 0).astype(jnp.bfloat16)
        g2 = jnp.concatenate(
            [jnp.where(low, g, 0.0), jnp.where(low, 0.0, g)], 0).astype(jnp.bfloat16)
        q_tags = tag_rows[pl.ds(tile, 1), :]

        def score_step(j, peak):
            keys = pl.ds(pl.multiple_of(key0 + j * TK, LANES), TK)
            held = pl.ds(pl.multiple_of(j * TK, TK), TK)
            s = dot_nt(k_ref[keys, :], q2)
            same = tag_cols[keys, :] == q_tags
            s = jnp.concatenate(
                [jnp.where(same, s[:, :TQ], -1e30), jnp.where(same, s[:, TQ:], -1e30)], 1)
            s_buf[held, :] = s
            dp_buf[held, :] = dot_nt(v_ref[keys, :], g2)
            return jnp.maximum(peak, jnp.max(s.reshape(TK // 8, 8, 2 * TQ), 0))

        peak = lax.fori_loop(0, steps, score_step, jnp.full((8, 2 * TQ), -1e30, jnp.float32))
        peak = jnp.max(peak, 0, keepdims=True)

        def weight_step(j, sums):
            total, delta = sums
            held = pl.ds(pl.multiple_of(j * TK, TK), TK)
            w = jnp.exp(s_buf[held, :] - peak)
            s_buf[held, :] = w
            wd = w * dp_buf[held, :]
            total = total + jnp.sum(w.reshape(TK // 8, 8, 2 * TQ), 0)
            delta = delta + jnp.sum(wd.reshape(TK // 8, 8, 2 * TQ), 0)
            return total, delta

        zero = jnp.zeros((8, 2 * TQ), jnp.float32)
        total, delta = lax.fori_loop(0, steps, weight_step, (zero, zero))
        inverse = 1.0 / jnp.sum(total, 0, keepdims=True)
        delta = jnp.sum(delta, 0, keepdims=True) * inverse
        att_acc[...] = jnp.zeros_like(att_acc)
        dq_acc[...] = jnp.zeros_like(dq_acc)

        def grad_step(j, c):
            keys = pl.ds(pl.multiple_of(key0 + j * TK, LANES), TK)
            held = pl.ds(pl.multiple_of(j * TK, TK), TK)
            p = s_buf[held, :] * inverse
            ds = (p * (dp_buf[held, :] - delta)).astype(jnp.bfloat16)
            p = p.astype(jnp.bfloat16)
            att_acc[...] += dot_nn(vt_ref[:, keys], p)
            dq_acc[...] += dot_nn(kt_ref[:, keys], ds)
            dv_acc[keys, :] += dot_nn(p, g2)
            dk_acc[keys, :] += dot_nn(ds, q2)
            return c

        lax.fori_loop(0, steps, grad_step, 0)
        att = att_acc[...]
        dq = dq_acc[...] * scale
        top = lax.broadcasted_iota(jnp.int32, (LANES, TQ), 0) < HEAD_DIM
        att_ref[rows, :] = jnp.where(top, att[:, :TQ], att[:, TQ:]).T.astype(jnp.bfloat16)
        dq_ref[rows, :] = jnp.where(top, dq[:, :TQ], dq[:, TQ:]).T.astype(jnp.bfloat16)
        return carry

    lax.fori_loop(bounds[0], bounds[1], one_tile, 0)
    dk_ref[...] = dk_acc[...].astype(jnp.bfloat16)
    dv_ref[...] = dv_acc[...].astype(jnp.bfloat16)


def attend(q, k, v, g, tags, bounds, halo):
    width = q.shape[0]
    most = 2 * halo + TQ + 2 * TK
    span = -(-min(most, width + TK) // TK) * TK
    vmem = pl.BlockSpec(memory_space=pltpu.VMEM)
    smem = pl.BlockSpec(memory_space=pltpu.SMEM)
    out = jax.ShapeDtypeStruct((width, LANES), jnp.bfloat16)
    return pl.pallas_call(
        attend_kernel,
        out_shape=(out,) * 4,
        in_specs=[smem, smem] + [vmem] * 8,
        out_specs=(vmem,) * 4,
        scratch_shapes=[
            pltpu.VMEM((span, 2 * TQ), jnp.float32),
            pltpu.VMEM((span, 2 * TQ), jnp.float32),
            pltpu.VMEM((width, LANES), jnp.float32),
            pltpu.VMEM((width, LANES), jnp.float32),
            pltpu.VMEM((LANES, 2 * TQ), jnp.float32),
            pltpu.VMEM((LANES, 2 * TQ), jnp.float32),
        ],
        compiler_params=pltpu.CompilerParams(vmem_limit_bytes=56 * 1024 * 1024),
        cost_estimate=pl.CostEstimate(
            flops=60_000_000_000, bytes_accessed=12_000_000, transcendentals=8_000_000),
    )(tags, bounds, q, k, v, g, k.T, v.T,
      jnp.broadcast_to(tags[:, None], (width, LANES)), tags.reshape(width // LANES, LANES))


def shards(queries, keys, values, out_grad, image_ids):
    row_count, features = queries.shape
    count = lax.axis_size("img")
    team = features // LANES
    groups = [list(range(at, at + team)) for at in range(0, count, team)]
    own = team * row_count
    halo = REACH * row_count
    down = [(i, i - team) for i in range(team, count)]
    up = [(i, i + team) for i in range(count - team)]

    def gather(x):
        x = x.reshape(row_count, team, LANES).transpose(1, 0, 2)
        x = lax.all_to_all(x, "img", 0, 0, axis_index_groups=groups)
        x = x.reshape(own, LANES)
        far = lax.ppermute(x[:halo], "img", down)
        return jnp.concatenate([x, far, jnp.zeros((TK - LANES, LANES), x.dtype)], 0)

    tags = lax.all_gather(image_ids, "img", tiled=True) + 1
    start = (lax.axis_index("img") // team) * own
    padded = jnp.concatenate(
        [jnp.zeros((1,), jnp.int32), tags, jnp.full((halo + TK - LANES,), NO_TAG, jnp.int32)])
    width = own + halo + TK - LANES
    before = lax.dynamic_slice_in_dim(padded, start, 1)[0]
    window = lax.dynamic_slice_in_dim(padded, start + 1, width)
    window = jnp.where(jnp.arange(width) < own + halo, window, NO_TAG)
    first = jnp.sum((window == before).astype(jnp.int32))
    last = jnp.sum((window <= window[own - 1]).astype(jnp.int32))
    bounds = jnp.stack([first // TQ, (last + TQ - 1) // TQ]).astype(jnp.int32)

    results = attend(*(gather(x) for x in (queries, keys, values, out_grad)), window, bounds, halo)
    from_below = (window[:halo] == before)[:, None]

    def give_back(x):
        far = lax.ppermute(x[own : own + halo], "img", up)
        x = jnp.concatenate([jnp.where(from_below, far, x[:halo]), x[halo:own]], 0)
        x = lax.all_to_all(
            x.reshape(team, row_count, LANES), "img", 0, 0, axis_index_groups=groups)
        return x.transpose(1, 0, 2).reshape(row_count, features)

    return tuple(give_back(x) for x in results)


def solution(mesh):
    in_specs = (P("img", None), P("img", None), P("img", None), P("img", None), P("img"))
    out_specs = (P("img", None), P("img", None), P("img", None), P("img", None))
    return jax.shard_map(shards, mesh=mesh, in_specs=in_specs, out_specs=out_specs, check_vma=False)
```

time: 753 us -> 327 us (0.43)
  waiting for transfers between devices: 276 us -> 75 us
  starting transfers between devices: 189 us -> 68.7 us
  local copies, waits for them, and re-layouts: 151 us -> 34.3 us
  matrix products: 103 us -> 0 us
  blocking collectives: 0 us -> 75.3 us
  Pallas kernels: 0 us -> 51.6 us
  other arithmetic: 26.6 us -> 17.9 us
    ppermute x30 -> x8, waiting for transfers between devices: 276 us -> 23.1 us  [the longest x4 14.4 us: give_back(): far = lax.ppermute(x[own:own + halo], 'img', up)]
    ppermute x30 -> x8, starting transfers between devices: 189 us -> 45.1 us  [the longest x4 40 us: give_back(): far = lax.ppermute(x[own:own + halo], 'img', up)]
    dot_general x40 -> x0, matrix products: 81.7 us -> none  [the longest x8 29.7 us: turn(): jnp.einsum('hrw,rhd->whd', probs_b, grad_cols, preferred_element_type=jnp...]
    all_to_all x0 -> x6, waiting for transfers between devices: none -> 52 us  [the longest x4 33.2 us: gather(): x = lax.all_to_all(x, 'img', 0, 0, axis_index_groups=groups)]
    pallas_call x0 -> x1, Pallas kernels: none -> 51.6 us  [attend(): pl.pallas_call(attend_kernel, out_shape=(out,) * 4, in_specs=[smem, smem]...]
    dynamic_slice x48 -> x1, local copies, waits for them, and re-layouts: 46.9 us -> 0.61 us  [shards(): before = lax.dynamic_slice_in_dim(padded, start, 1)[0]]
    all_gather x0 -> x1, blocking collectives: none -> 44.7 us  [shards(): tags = lax.all_gather(image_ids, 'img', tiled=True) + 1]
    all_to_all x0 -> x2, blocking collectives: none -> 30.5 us  [give_back(): lax.all_to_all(x.reshape(team, row_count, LANES), 'img', 0, 0, axis_index...]
  transfers between devices with their start and end apart: 30 -> 14, of which waited for: 12 -> 10; matrix products, arithmetic and copies ran while one was open for 6% -> 11% of each run, Pallas kernels for 0% -> 0%
where the time goes in v1:
time: 327 us
  blocking collectives  75.3 us (23%)
  waiting for transfers between devices  75 us (23%)
  starting transfers between devices  68.7 us (21%)
  Pallas kernels  51.6 us (16%)
  local copies, waits for them, and re-layouts  34.3 us (10%)
  other arithmetic  17.9 us (5%)
  between operations  4.22 us (1%)
    pallas_call x1, Pallas kernels, attend(): pl.pallas_call(attend_kernel, out_shape=(out,) * 4, in_specs=[smem, smem]...  51.6 us
    all_gather x1, blocking collectives, shards(): tags = lax.all_gather(image_ids, 'img', tiled=True) + 1  44.7 us
    ppermute x4, starting transfers between devices, give_back(): far = lax.ppermute(x[own:own + halo], 'img', up)  40 us
    all_to_all x4, waiting for transfers between devices, gather(): x = lax.all_to_all(x, 'img', 0, 0, axis_index_groups=groups)  33.2 us
    all_to_all x2, blocking collectives, give_back(): lax.all_to_all(x.reshape(team, row_count, LANES), 'img', 0, 0, axis_index...  30.5 us
    all_to_all x2, waiting for transfers between devices, give_back(): lax.all_to_all(x.reshape(team, row_count, LANES), 'img', 0, 0, axis_index...  18.8 us
    all_to_all x4, starting transfers between devices, gather(): x = lax.all_to_all(x, 'img', 0, 0, axis_index_groups=groups)  16.5 us
    ppermute x4, waiting for transfers between devices, give_back(): far = lax.ppermute(x[own:own + halo], 'img', up)  14.4 us
  transfers between devices with their start and end apart: 14, of which 10 were waited for; matrix products, arithmetic and copies ran while one was open for 11% of the time, Pallas kernels for 0%

profile of v1, /device:TPU:0, one launch (start us, length us, event | category | flops | bytes accessed | tf_op | source)
XLA Modules:
  0.0 327.0 jit_solution(17023546462459648491)
XLA Ops:
  0.7 2.4 copy.55
  3.1 5.2 %all-to-all-start.1 = ((bf16[8,384,128]{1,2,0:T(8,128)(2,1)}), bf16[8,384,128]{1,2,0:T(8,128)(2,1)S(1)}, u32[]{:S(2)}, u32[]{:S(2)}) async-start(bf16[8,384,128]{1,2,0:T(8,128)(2,1)} %bitcast.9), calls=%async_computation.1 | async-start | bytes 1572864 | tf_op jit(solution)/shard_map/all_to_all | solution.py:149
  8.3 1.2 copy.59
  9.4 11.4 %all-to-all-done.1 = bf16[8,384,128]{1,2,0:T(8,128)(2,1)S(1)} async-done(((bf16[8,384,128]{1,2,0:T(8,128)(2,1)}), bf16[8,384,128]{1,2,0:T(8,128)(2,1)S(1)}, u32[]{:S(2)}, u32[]{:S(2)}) %all-to-all-start.1) | async-done | bytes 786464 | tf_op jit(solution)/shard_map/all_to_all | solution.py:149
  20.8 3.5 %all-to-all-start.2 = ((bf16[8,384,128]{1,2,0:T(8,128)(2,1)}), bf16[8,384,128]{1,2,0:T(8,128)(2,1)S(1)}, u32[]{:S(2)}, u32[]{:S(2)}) async-start(bf16[8,384,128]{1,2,0:T(8,128)(2,1)} %bitcast.12), calls=%async_computation.2 | async-start | bytes 1572864 | tf_op jit(solution)/shard_map/all_to_all | solution.py:149
  24.4 1.0 bitcast_bitcast_fusion.1
  25.4 11.5 %all-to-all-done.2 = bf16[8,384,128]{1,2,0:T(8,128)(2,1)S(1)} async-done(((bf16[8,384,128]{1,2,0:T(8,128)(2,1)}), bf16[8,384,128]{1,2,0:T(8,128)(2,1)S(1)}, u32[]{:S(2)}, u32[]{:S(2)}) %all-to-all-start.2) | async-done | bytes 786464 | tf_op jit(solution)/shard_map/all_to_all | solution.py:149
  36.9 3.5 %all-to-all-start = ((bf16[8,384,128]{2,1,0:T(8,128)(2,1)}), bf16[8,384,128]{2,1,0:T(8,128)(2,1)S(1)}, u32[]{:S(2)}, u32[]{:S(2)}) async-start(bf16[8,384,128]{2,1,0:T(8,128)(2,1)} %bitcast_bitcast_fusion.1), calls=%async_computation | async-start | bytes 1572864 | tf_op jit(solution)/shard_map/all_to_all | solution.py:149
  40.5 2.2 bitcast_bitcast_fusion
  42.6 10.3 %all-to-all-done = bf16[8,384,128]{2,1,0:T(8,128)(2,1)S(1)} async-done(((bf16[8,384,128]{2,1,0:T(8,128)(2,1)}), bf16[8,384,128]{2,1,0:T(8,128)(2,1)S(1)}, u32[]{:S(2)}, u32[]{:S(2)}) %all-to-all-start) | async-done | bytes 786464 | tf_op jit(solution)/shard_map/all_to_all | solution.py:149
  52.9 4.2 %all-to-all-start.3 = ((bf16[8,384,128]{2,1,0:T(8,128)(2,1)}), bf16[8,384,128]{2,1,0:T(8,128)(2,1)}, u32[]{:S(2)}, u32[]{:S(2)}) async-start(bf16[8,384,128]{2,1,0:T(8,128)(2,1)} %bitcast_bitcast_fusion), calls=%async_computation.3 | async-start | bytes 1572864 | tf_op jit(solution)/shard_map/all_to_all | solution.py:149
  57.2 44.7 %all-gather = s32[32,1,384]{2,1,0:T(1,128)S(1)} all-gather(s32[1,1,384]{2,1,0:T(1,128)S(1)} %reshape.82), channel_id=1, replica_groups=mesh['img'=32] {'img'}, dimensions={0}, use_global_device_ids=true | all-gather | bytes 50688 | tf_op jit(solution)/shard_map/all_gather | solution.py:154
  102.7 0.7 slice.91
  103.5 1.2 copy.57
  104.6 0.9 copy.58
  105.5 1.3 collective-permute-start.1
  106.8 0.7 slice.92
  107.6 1.2 copy.61
  108.7 0.9 copy.62
  109.6 1.3 collective-permute-start.2
  111.6 2.0 convert_reduce_fusion.1
  116.9 0.7 pad_add_fusion.bounds
  117.6 0.7 fusion.2.tag_rows
  118.2 1.0 copy.73
  119.2 1.0 copy.74
  120.2 0.7 slice.90
  121.0 1.3 collective-permute-start
  122.3 1.7 slice.93
  124.0 1.3 collective-permute-start.3
  125.3 3.2 fusion
  128.5 1.4 copy.65.k_ref
  130.0 1.4 copy.66.v_ref
  131.4 3.0 collective-permute-done
  134.3 5.7 %collective-permute-done.3 = bf16[1152,128]{1,0:T(8,128)(2,1)} collective-permute-done((bf16[1152,128]{1,0:T(8,128)(2,1)}, bf16[1152,128]{1,0:T(8,128)(2,1)}, u32[]{:S(2)}, u32[]{:S(2)}) %collective-permute-start.3) | collective-permute-done | bytes 294944 | tf_op jit(solution)/shard_map/ppermute | solution.py:151
  140.0 5.8 %maximum_maximum_fusion.3 = (bf16[4352,128]{1,0:T(8,128)(2,1)}, bf16[4352,128]{1,0:T(8,128)(2,1)}) fusion(bf16[1152,128]{1,0:T(8,128)(2,1)} %collective-permute-done.3, bf16[3072,128]{1,0:T(8,128)(2,1)} %bitcast.15, bf16[4352]{0:T(1024)(128)(2,1)S(1)} %pad.19.clone, bf16[1152,128]{1,0:T(8,128)(2,1)} %collective-permute-done, bf16[3072,128]{1,0:T(8,128)(2,1)S(1)} %bitcast.71), kind=kLoop, calls=%fused_computation.3 | loop fusion | flops 6127616 | bytes 4399616 | tf_op jit(solution)/shard_map/concatenate | solution.py:152
  145.8 3.0 broadcast_in_dim.34.tag_cols
  148.8 51.6 %shard_map.84 = (bf16[4352,128]{1,0:T(8,128)(2,1)}, bf16[4352,128]{1,0:T(8,128)(2,1)}, bf16[4352,128]{1,0:T(8,128)(2,1)}, bf16[4352,128]{1,0:T(8,128)(2,1)}) custom-call(s32[4352]{0:T(1024)} %copy-done.8, s32[2]{0:T(128)} %pad_add_fusion.bounds, bf16[4352,128]{1,0:T(8,128)(2,1)} %get-tuple-element.21.q_ref, bf16[4352,128]{1,0:T(8,128)(2,1)} %copy.65.k_ref, ...), custom_call_target="tpu_custom_call" | custom-call | flops 60000002048 | bytes 12000000 | tf_op jit(solution)/shard_map/pallas_call | solution.py:117
  200.4 1.1 slice.76
  201.6 34.2 %collective-permute-start.4 = (bf16[1152,128]{1,0:T(8,128)(2,1)S(1)}, bf16[1152,128]{1,0:T(8,128)(2,1)S(1)}, u32[]{:S(2)}, u32[]{:S(2)}) collective-permute-start(bf16[1152,128]{1,0:T(8,128)(2,1)S(1)} %slice.76), channel_id=1, source_target_pairs={{0,8},{1,9},{2,10},{3,11},{4,12},{5,13},{6,14},{7,15},{8,16},{9,17... | collective-permute-start | bytes 884744 | tf_op jit(solution)/shard_map/ppermute | solution.py:170
  235.8 1.0 slice.79
  236.8 1.9 collective-permute-start.5
  238.7 1.0 slice.82
  239.7 1.9 collective-permute-start.6
  241.6 1.0 slice.85
  242.6 1.9 collective-permute-start.7
  244.5 1.3 slice_compare_fusion
  245.9 3.5 %collective-permute-done.5 = bf16[1152,128]{1,0:T(8,128)(2,1)S(1)} collective-permute-done((bf16[1152,128]{1,0:T(8,128)(2,1)S(1)}, bf16[1152,128]{1,0:T(8,128)(2,1)S(1)}, u32[]{:S(2)}, u32[]{:S(2)}) %collective-permute-start.5) | collective-permute-done | bytes 294944 | tf_op jit(solution)/shard_map/ppermute | solution.py:170
  249.4 6.3 %collective-permute-done.6 = bf16[1152,128]{1,0:T(8,128)(2,1)S(1)} collective-permute-done((bf16[1152,128]{1,0:T(8,128)(2,1)S(1)}, bf16[1152,128]{1,0:T(8,128)(2,1)S(1)}, u32[]{:S(2)}, u32[]{:S(2)}) %collective-permute-start.6) | collective-permute-done | bytes 294944 | tf_op jit(solution)/shard_map/ppermute | solution.py:170
  255.8 4.6 %collective-permute-done.7 = bf16[1152,128]{1,0:T(8,128)(2,1)S(1)} collective-permute-done((bf16[1152,128]{1,0:T(8,128)(2,1)S(1)}, bf16[1152,128]{1,0:T(8,128)(2,1)S(1)}, u32[]{:S(2)}, u32[]{:S(2)}) %collective-permute-start.7) | collective-permute-done | bytes 294944 | tf_op jit(solution)/shard_map/ppermute | solution.py:170
  260.3 2.0 slice_select_fusion
  262.4 1.0 pad_maximum_fusion.2
  263.4 14.9 %all_to_all.40 = bf16[8,384,128]{2,1,0:T(8,128)(2,1)S(1)} all-to-all(bf16[8,384,128]{2,1,0:T(8,128)(2,1)S(1)} %bitcast.76), channel_id=1, replica_groups={{0,1,2,3,4,5,6,7},{8,9,10,11,12,13,14,15},{16,17,18,19,20,21,22,23},{24..., dimensions={0} | all-to-all | bytes 1572864 | tf_op jit(solution)/shard_map/all_to_all | solution.py:172
  278.3 3.5 %all-to-all-start.6 = ((bf16[8,384,128]{2,1,0:T(8,128)(2,1)}), bf16[8,384,128]{2,1,0:T(8,128)(2,1)S(1)}, u32[]{:S(2)}, u32[]{:S(2)}) async-start(bf16[8,384,128]{2,1,0:T(8,128)(2,1)} %bitcast.24), calls=%async_computation.6 | async-start | bytes 1572864 | tf_op jit(solution)/shard_map/all_to_all | solution.py:172
  281.8 1.1 slice.78
  283.0 1.1 slice.81
  284.0 1.0 pad_maximum_fusion
  285.1 9.3 %all-to-all-done.6 = bf16[8,384,128]{2,1,0:T(8,128)(2,1)S(1)} async-done(((bf16[8,384,128]{2,1,0:T(8,128)(2,1)}), bf16[8,384,128]{2,1,0:T(8,128)(2,1)S(1)}, u32[]{:S(2)}, u32[]{:S(2)}) %all-to-all-start.6) | async-done | bytes 786464 | tf_op jit(solution)/shard_map/all_to_all | solution.py:172
  294.3 15.6 %all_to_all.41 = bf16[8,384,128]{2,1,0:T(8,128)(2,1)} all-to-all(bf16[8,384,128]{2,1,0:T(8,128)(2,1)S(1)} %bitcast.75), channel_id=1, replica_groups={{0,1,2,3,4,5,6,7},{8,9,10,11,12,13,14,15},{16,17,18,19,20,21,22,23},{24..., dimensions={0} | all-to-all | bytes 1572864 | tf_op jit(solution)/shard_map/all_to_all | solution.py:172
  310.0 3.5 %all-to-all-start.4 = ((bf16[8,384,128]{2,1,0:T(8,128)(2,1)}), bf16[8,384,128]{2,1,0:T(8,128)(2,1)S(1)}, u32[]{:S(2)}, u32[]{:S(2)}) async-start(bf16[8,384,128]{2,1,0:T(8,128)(2,1)} %bitcast.74), calls=%async_computation.4 | async-start | bytes 1572864 | tf_op jit(solution)/shard_map/all_to_all | solution.py:172
  313.5 1.0 copy_bitcast_fusion
  314.5 1.0 copy_bitcast_fusion.1
  315.5 1.0 copy_bitcast_fusion.2
  316.5 9.5 %all-to-all-done.4 = bf16[8,384,128]{2,1,0:T(8,128)(2,1)S(1)} async-done(((bf16[8,384,128]{2,1,0:T(8,128)(2,1)}), bf16[8,384,128]{2,1,0:T(8,128)(2,1)S(1)}, u32[]{:S(2)}, u32[]{:S(2)}) %all-to-all-start.4) | async-done | bytes 786464 | tf_op jit(solution)/shard_map/all_to_all | solution.py:172
  326.0 1.0 copy_bitcast_fusion.3
  (35 shorter events, 1.6 us)
Async XLA Ops:
  0.6 23.7 %copy-start = (bf16[384,1024]{1,0:T(8,128)(2,1)S(1)}, bf16[384,1024]{1,0:T(8,128)(2,1)}, u32[]{:S(2)}) copy-start(bf16[384,1024]{1,0:T(8,128)(2,1)} %param.5) | copy-start | bytes 2359300
  0.6 7.6 %copy-start.7 = (bf16[384,1024]{1,0:T(8,128)(2,1)S(1)}, bf16[384,1024]{1,0:T(8,128)(2,1)}, u32[]{:S(2)}) copy-start(bf16[384,1024]{1,0:T(8,128)(2,1)} %param.7) | copy-start | bytes 2359300
  3.1 17.8 %all-to-all-start.1 = ((bf16[8,384,128]{1,2,0:T(8,128)(2,1)}), bf16[8,384,128]{1,2,0:T(8,128)(2,1)S(1)}, u32[]{:S(2)}, u32[]{:S(2)}) async-start(bf16[8,384,128]{1,2,0:T(8,128)(2,1)} %bitcast.9), calls=%async_computation.1 | async-start | bytes 1572864 | tf_op jit(solution)/shard_map/all_to_all | solution.py:149
  20.8 16.1 %all-to-all-start.2 = ((bf16[8,384,128]{1,2,0:T(8,128)(2,1)}), bf16[8,384,128]{1,2,0:T(8,128)(2,1)S(1)}, u32[]{:S(2)}, u32[]{:S(2)}) async-start(bf16[8,384,128]{1,2,0:T(8,128)(2,1)} %bitcast.12), calls=%async_computation.2 | async-start | bytes 1572864 | tf_op jit(solution)/shard_map/all_to_all | solution.py:149
  36.9 16.1 %all-to-all-start = ((bf16[8,384,128]{2,1,0:T(8,128)(2,1)}), bf16[8,384,128]{2,1,0:T(8,128)(2,1)S(1)}, u32[]{:S(2)}, u32[]{:S(2)}) async-start(bf16[8,384,128]{2,1,0:T(8,128)(2,1)} %bitcast_bitcast_fusion.1), calls=%async_computation | async-start | bytes 1572864 | tf_op jit(solution)/shard_map/all_to_all | solution.py:149
  40.4 16.8 %copy-start.9 = (s32[384]{0:T(512)S(1)}, s32[384]{0:T(512)}, u32[]{:S(2)}) copy-start(s32[384]{0:T(512)} %param.9) | copy-start | bytes 4612
  52.9 67.3 %copy-start.1 = (bf16[8,384,128]{2,1,0:T(8,128)(2,1)}, bf16[8,384,128]{2,1,0:T(8,128)(2,1)S(1)}, u32[]{:S(2)}) copy-start(bf16[8,384,128]{2,1,0:T(8,128)(2,1)S(1)} %all-to-all-done) | copy-start | bytes 2359300
  52.9 69.3 %all-to-all-start.3 = ((bf16[8,384,128]{2,1,0:T(8,128)(2,1)}), bf16[8,384,128]{2,1,0:T(8,128)(2,1)}, u32[]{:S(2)}, u32[]{:S(2)}) async-start(bf16[8,384,128]{2,1,0:T(8,128)(2,1)} %bitcast_bitcast_fusion), calls=%async_computation.3 | async-start | bytes 1572864 | tf_op jit(solution)/shard_map/all_to_all | solution.py:149
  105.5 19.7 %collective-permute-start.1 = (bf16[1152,128]{0,1:T(8,128)(2,1)}, bf16[1152,128]{0,1:T(8,128)(2,1)}, u32[]{:S(2)}, u32[]{:S(2)}) collective-permute-start(bf16[1152,128]{0,1:T(8,128)(2,1)} %copy.58), channel_id=1, source_target_pairs={{8,0},{9,1},{10,2},{11,3},{12,4},{13,5},{14,6},{15,7},{16,8},{17,9... | collective-permute-start | bytes 884744 | tf_op jit(solution)/shard_map/ppermute | solution.py:151
  109.6 15.7 %collective-permute-start.2 = (bf16[1152,128]{0,1:T(8,128)(2,1)}, bf16[1152,128]{0,1:T(8,128)(2,1)S(1)}, u32[]{:S(2)}, u32[]{:S(2)}) collective-permute-start(bf16[1152,128]{0,1:T(8,128)(2,1)} %copy.62), channel_id=1, source_target_pairs={{8,0},{9,1},{10,2},{11,3},{12,4},{13,5},{14,6},{15,7},{16,8},{17,9... | collective-permute-start | bytes 884744 | tf_op jit(solution)/shard_map/ppermute | solution.py:151
  111.0 34.8 %copy-start.8 = (s32[4352]{0:T(1024)}, s32[4352]{0:T(1024)S(1)}, u32[]{:S(2)}) copy-start(s32[4352]{0:T(1024)S(1)} %dynamic-slice_select_fusion.tags_s) | copy-start | bytes 52228
  121.0 13.3 %collective-permute-start = (bf16[1152,128]{1,0:T(8,128)(2,1)}, bf16[1152,128]{1,0:T(8,128)(2,1)}, u32[]{:S(2)}, u32[]{:S(2)}) collective-permute-start(bf16[1152,128]{1,0:T(8,128)(2,1)} %bitcast.7), channel_id=1, source_target_pairs={{8,0},{9,1},{10,2},{11,3},{12,4},{13,5},{14,6},{15,7},{16,8},{17,9... | collective-permute-start | bytes 884744 | tf_op jit(solution)/shard_map/ppermute | solution.py:151
  124.0 16.0 %collective-permute-start.3 = (bf16[1152,128]{1,0:T(8,128)(2,1)}, bf16[1152,128]{1,0:T(8,128)(2,1)}, u32[]{:S(2)}, u32[]{:S(2)}) collective-permute-start(bf16[1152,128]{1,0:T(8,128)(2,1)} %bitcast.16), channel_id=1, source_target_pairs={{8,0},{9,1},{10,2},{11,3},{12,4},{13,5},{14,6},{15,7},{16,8},{17,9... | collective-permute-start | bytes 884744 | tf_op jit(solution)/shard_map/ppermute | solution.py:151
  130.0 10.1 %copy-start.2 = (bf16[8,384,128]{2,1,0:T(8,128)(2,1)S(1)}, bf16[8,384,128]{2,1,0:T(8,128)(2,1)}, u32[]{:S(2)}) copy-start(bf16[8,384,128]{2,1,0:T(8,128)(2,1)} %copy-done.1) | copy-start | bytes 2359300
  200.4 45.4 %copy-start.5 = (bf16[4352,128]{1,0:T(8,128)(2,1)S(1)}, bf16[4352,128]{1,0:T(8,128)(2,1)}, u32[]{:S(2)}) copy-start(bf16[4352,128]{1,0:T(8,128)(2,1)} %get-tuple-element.10) | copy-start | bytes 3342340
  200.4 45.5 %copy-start.6 = (bf16[4352,128]{1,0:T(8,128)(2,1)S(1)}, bf16[4352,128]{1,0:T(8,128)(2,1)}, u32[]{:S(2)}) copy-start(bf16[4352,128]{1,0:T(8,128)(2,1)} %get-tuple-element.11) | copy-start | bytes 3342340
  201.6 44.4 %collective-permute-start.4 = (bf16[1152,128]{1,0:T(8,128)(2,1)S(1)}, bf16[1152,128]{1,0:T(8,128)(2,1)S(1)}, u32[]{:S(2)}, u32[]{:S(2)}) collective-permute-start(bf16[1152,128]{1,0:T(8,128)(2,1)S(1)} %slice.76), channel_id=1, source_target_pairs={{0,8},{1,9},{2,10},{3,11},{4,12},{5,13},{6,14},{7,15},{8,16},{9,17... | collective-permute-start | bytes 884744 | tf_op jit(solution)/shard_map/ppermute | solution.py:170
  236.8 12.7 %collective-permute-start.5 = (bf16[1152,128]{1,0:T(8,128)(2,1)S(1)}, bf16[1152,128]{1,0:T(8,128)(2,1)S(1)}, u32[]{:S(2)}, u32[]{:S(2)}) collective-permute-start(bf16[1152,128]{1,0:T(8,128)(2,1)S(1)} %slice.79), channel_id=1, source_target_pairs={{0,8},{1,9},{2,10},{3,11},{4,12},{5,13},{6,14},{7,15},{8,16},{9,17... | collective-permute-start | bytes 884744 | tf_op jit(solution)/shard_map/ppermute | solution.py:170
  239.7 16.1 %collective-permute-start.6 = (bf16[1152,128]{1,0:T(8,128)(2,1)S(1)}, bf16[1152,128]{1,0:T(8,128)(2,1)S(1)}, u32[]{:S(2)}, u32[]{:S(2)}) collective-permute-start(bf16[1152,128]{1,0:T(8,128)(2,1)S(1)} %slice.82), channel_id=1, source_target_pairs={{0,8},{1,9},{2,10},{3,11},{4,12},{5,13},{6,14},{7,15},{8,16},{9,17... | collective-permute-start | bytes 884744 | tf_op jit(solution)/shard_map/ppermute | solution.py:170
  242.6 17.7 %collective-permute-start.7 = (bf16[1152,128]{1,0:T(8,128)(2,1)S(1)}, bf16[1152,128]{1,0:T(8,128)(2,1)S(1)}, u32[]{:S(2)}, u32[]{:S(2)}) collective-permute-start(bf16[1152,128]{1,0:T(8,128)(2,1)S(1)} %slice.85), channel_id=1, source_target_pairs={{0,8},{1,9},{2,10},{3,11},{4,12},{5,13},{6,14},{7,15},{8,16},{9,17... | collective-permute-start | bytes 884744 | tf_op jit(solution)/shard_map/ppermute | solution.py:170
  278.3 16.1 %all-to-all-start.6 = ((bf16[8,384,128]{2,1,0:T(8,128)(2,1)}), bf16[8,384,128]{2,1,0:T(8,128)(2,1)S(1)}, u32[]{:S(2)}, u32[]{:S(2)}) async-start(bf16[8,384,128]{2,1,0:T(8,128)(2,1)} %bitcast.24), calls=%async_computation.6 | async-start | bytes 1572864 | tf_op jit(solution)/shard_map/all_to_all | solution.py:172
  281.8 2.2 copy-start.4
  310.0 16.1 %all-to-all-start.4 = ((bf16[8,384,128]{2,1,0:T(8,128)(2,1)}), bf16[8,384,128]{2,1,0:T(8,128)(2,1)S(1)}, u32[]{:S(2)}, u32[]{:S(2)}) async-start(bf16[8,384,128]{2,1,0:T(8,128)(2,1)} %bitcast.74), calls=%async_computation.4 | async-start | bytes 1572864 | tf_op jit(solution)/shard_map/all_to_all | solution.py:172
  313.5 2.0 copy-start.3
